TPU v7x, 1024 devices: a whole 4x8x16 slice. The times are simulated.
1024 devices in a mesh: own: 16 (over y, x_hi), rep: 64 (over x_lo, z, core).
Axes of the slice: x: 4 (x_hi: 2, x_lo: 2; x = x_hi * 2 + x_lo), y: 8, z: 16, core: 2. Of those that a mesh axis runs over, the one named last changes fastest.
Arguments:
- tokens: bfloat16 [131072, 2048], P(('own', 'rep')), may hold values from -6 to 6
- cotangent: bfloat16 [131072, 2048], P(('own', 'rep')), may hold values from -3 to 3
- route: int32 [131072, 1], P(('own', 'rep')), may hold values from 0 to 63; in each aligned block of 128 rows (0 to 127, 128 to 255, ...) at most 3 rows name the same one
- host: int32 [64], replicated, may hold values from 0 to 63, each once
- w_gate: bfloat16 [64, 2048, 256], P('rep', 'own'), may hold values from -0.125 to 0.125
- w_up: bfloat16 [64, 2048, 256], P('rep', 'own'), may hold values from -0.125 to 0.125
- w_down_t: bfloat16 [64, 2048, 256], P('rep', 'own'), may hold values from -0.375 to 0.375
Outputs:
- x_grad: bfloat16 [131072, 2048], P(('own', 'rep'))
- grad_gate: float32 [64, 2048, 256], P('rep', 'own')
- grad_up: float32 [64, 2048, 256], P('rep', 'own')
- grad_down_t: float32 [64, 2048, 256], P('rep', 'own')
Inputs may be any that keep to these rules, and one draw needn't show every extreme that they name: `route`: among the 128 tokens of one device no hot expert is named more than 3 times, and in every draw some expert is named exactly 3 times on some device. `host`: each replica group serves exactly one hot expert.
All inputs are finite; a program needn't handle non-finite values.
Results may differ from a plain program's by a relative error of at most 0.017.
Values may be sent and summed in bfloat16 or wider, within the bound.
A program may use at most 32 MiB of HBM per device.

v0:
```python
import jax
import jax.numpy as jnp
from jax import lax
from jax.sharding import PartitionSpec as P


def times_rows(left, right):
    return lax.dot_general(
        left, right, (((1,), (1,)), ((), ())), preferred_element_type=jnp.float32
    )


def first_contract(left, right):
    return lax.dot_general(
        left, right, (((0,), (0,)), ((), ())), preferred_element_type=jnp.float32
    )


def shards(tokens, cotangent, route, host, w_gate, w_up, w_down_t):
    tok_rows, model_width = tokens.shape
    hot_count = host.shape[0]
    hidden_width = w_gate.shape[2]
    capacity = max(2, (3 * tok_rows + 2 * hot_count - 1) // (2 * hot_count))
    slot_rows = hot_count * capacity
    labels = lax.broadcasted_iota(jnp.int32, (tok_rows, hot_count), 1)
    target = jnp.sum(jnp.where(route == labels, host[None, :], 0), axis=1)
    marked = (target[:, None] == labels).astype(jnp.int32)
    arrival = jnp.sum(jnp.cumsum(marked, axis=0) * marked, axis=1) - 1
    position = target * capacity + arrival
    slot_ids = lax.broadcasted_iota(jnp.int32, (slot_rows, tok_rows), 0)
    token_ids = lax.broadcasted_iota(jnp.int32, (slot_rows, tok_rows), 1)
    matched = slot_ids == position[None, :]
    filled = jnp.any(matched, axis=1)
    source_row = jnp.sum(jnp.where(matched, token_ids, 0), axis=1)
    zero_row = jnp.zeros((), jnp.bfloat16)
    send_x = jnp.where(filled[:, None], tokens[source_row], zero_row)
    send_dy = jnp.where(filled[:, None], cotangent[source_row], zero_row)
    recv_x, recv_dy = (
        lax.all_to_all(
            send_x.reshape(hot_count, capacity, model_width),
            "rep",
            split_axis=0,
            concat_axis=0,
            tiled=True,
        ),
        lax.all_to_all(
            send_dy.reshape(hot_count, capacity, model_width),
            "rep",
            split_axis=0,
            concat_axis=0,
            tiled=True,
        ),
    )
    slot_x = recv_x.reshape(slot_rows, model_width)
    slot_dy = recv_dy.reshape(slot_rows, model_width)
    gate_piece = w_gate[0]
    up_piece = w_up[0]
    down_piece = w_down_t[0]
    full_gate, full_up, full_down = (
        lax.all_gather(gate_piece, "own", axis=0, tiled=True),
        lax.all_gather(up_piece, "own", axis=0, tiled=True),
        lax.all_gather(down_piece, "own", axis=0, tiled=True),
    )
    gate_act = jnp.dot(slot_x, full_gate, preferred_element_type=jnp.float32)
    up_act = jnp.dot(slot_x, full_up, preferred_element_type=jnp.float32)
    back_grad = jnp.dot(slot_dy, full_down, preferred_element_type=jnp.float32)
    sigmoid_g = jax.nn.sigmoid(gate_act)
    silu_gate = gate_act * sigmoid_g
    hidden = (silu_gate * up_act).astype(jnp.bfloat16)
    grad_gate_h = (back_grad * up_act * sigmoid_g * (1.0 + gate_act * (1.0 - sigmoid_g))).astype(
        jnp.bfloat16
    )
    grad_up_h = (back_grad * silu_gate).astype(jnp.bfloat16)
    slot_grad = (times_rows(grad_gate_h, full_gate) + times_rows(grad_up_h, full_up)).astype(
        jnp.bfloat16
    )
    returned = lax.all_to_all(
        slot_grad.reshape(hot_count, capacity, model_width),
        "rep",
        split_axis=0,
        concat_axis=0,
        tiled=True,
    )
    x_grad = returned.reshape(slot_rows, model_width)[position]
    summed = lax.psum_scatter(
        jnp.concatenate(
            [
                first_contract(slot_x, grad_gate_h),
                first_contract(slot_x, grad_up_h),
                first_contract(slot_dy, hidden),
            ],
            axis=1,
        ).astype(jnp.bfloat16),
        "own",
        scatter_dimension=0,
        tiled=True,
    ).astype(jnp.float32)
    grad_gate = summed[:, :hidden_width][None]
    grad_up = summed[:, hidden_width : 2 * hidden_width][None]
    grad_down_t = summed[:, 2 * hidden_width :][None]
    return (x_grad, grad_gate, grad_up, grad_down_t)


def solution(mesh):
    return jax.shard_map(
        shards,
        mesh=mesh,
        in_specs=(
            P(("own", "rep"), None),
            P(("own", "rep"), None),
            P(("own", "rep"), None),
            P(),
            P("rep", "own", None),
            P("rep", "own", None),
            P("rep", "own", None),
        ),
        out_specs=(
            P(("own", "rep"), None),
            P("rep", "own", None),
            P("rep", "own", None),
            P("rep", "own", None),
        ),
        check_vma=False,
    )
```

profile of v0, /device:TPU:16, one launch (start us, length us, event | category | flops | bytes accessed | tf_op | source)
XLA Modules:
  0.0 572.8 jit_solution(10511624394873377351)
XLA Ops:
  7.2 0.9 select_reduce_fusion.2
  9.0 1.1 gather_fusion.1
  10.7 1.1 gather_fusion
  12.3 2.3 broadcast_select_fusion.1
  14.7 20.7 %all-to-all-start = ((bf16[64,3,2048]{2,1,0:T(4,128)(2,1)}), bf16[64,3,2048]{2,1,0:T(4,128)(2,1)S(1)}, u32[]{:S(2)}, u32[]{:S(2)}) async-start(bf16[64,3,2048]{2,1,0:T(4,128)(2,1)} %get-tuple-element.27), calls=%async_computation | async-start | bytes 2097152 | tf_op jit(solution)/shard_map/all_to_all | solution.py:46
  35.4 0.7 all-gather.11.cloned.1.call-update
  36.2 0.7 all-gather.9.cloned.1.call-update
  36.9 50.8 %all-to-all-done = bf16[64,3,2048]{2,1,0:T(4,128)(2,1)S(1)} async-done(((bf16[64,3,2048]{2,1,0:T(4,128)(2,1)}), bf16[64,3,2048]{2,1,0:T(4,128)(2,1)S(1)}, u32[]{:S(2)}, u32[]{:S(2)}) %all-to-all-start) | async-done | bytes 786464 | tf_op jit(solution)/shard_map/all_to_all | solution.py:46
  87.6 7.8 %all-to-all-start.1 = ((bf16[64,3,2048]{2,1,0:T(4,128)(2,1)}), bf16[64,3,2048]{2,1,0:T(4,128)(2,1)S(1)}, u32[]{:S(2)}, u32[]{:S(2)}) async-start(bf16[64,3,2048]{2,1,0:T(4,128)(2,1)} %get-tuple-element.28), calls=%async_computation.1 | async-start | bytes 2097152 | tf_op jit(solution)/shard_map/all_to_all | solution.py:39
  95.4 0.7 all-gather.7.cloned.1.call-update
  96.2 0.7 reshape.87
  96.9 50.7 %all-to-all-done.1 = bf16[64,3,2048]{2,1,0:T(4,128)(2,1)S(1)} async-done(((bf16[64,3,2048]{2,1,0:T(4,128)(2,1)}), bf16[64,3,2048]{2,1,0:T(4,128)(2,1)S(1)}, u32[]{:S(2)}, u32[]{:S(2)}) %all-to-all-start.1) | async-done | bytes 786464 | tf_op jit(solution)/shard_map/all_to_all | solution.py:39
  147.6 0.7 reshape.88
  148.3 1.6 fusion.3
  149.9 83.5 %all-gather.9.cloned.1.call-done = bf16[1,2048,256]{2,1,0:T(8,128)(2,1)} async-done(((bf16[1,128,256]{2,1,0:T(8,128)(2,1)}), bf16[1,2048,256]{2,1,0:T(8,128)(2,1)}) %all-gather.9.cloned.1.call-update) | async-done | bytes 1048592 | tf_op jit(solution)/shard_map/all_gather | solution.py:61
  233.5 1.6 fusion.6
  235.1 0.7 copy-done.4
  236.3 93.6 %all-gather.7.cloned.1.call-done = bf16[1,2048,256]{2,1,0:T(8,128)(2,1)} async-done(((bf16[1,128,256]{2,1,0:T(8,128)(2,1)}), bf16[1,2048,256]{2,1,0:T(8,128)(2,1)}) %all-gather.7.cloned.1.call-update) | async-done | bytes 1048592 | tf_op jit(solution)/shard_map/all_gather | solution.py:62
  329.9 1.6 multiply_convert_fusion.1
  332.7 1.9 pad_maximum_fusion
  334.5 4.6 copy.23
  339.2 1.2 copy-done.3
  341.4 1.3 reshape.89
  342.7 13.9 %all-to-all-start.2 = ((bf16[64,3,2048]{2,1,0:T(4,128)(2,1)}), bf16[64,3,2048]{2,1,0:T(4,128)(2,1)S(1)}, u32[]{:S(2)}, u32[]{:S(2)}) async-start(bf16[64,3,2048]{2,1,0:T(4,128)(2,1)} %reshape.89), calls=%async_computation.2 | async-start | bytes 2097152 | tf_op jit(solution)/shard_map/all_to_all | solution.py:77
  356.7 52.2 %all-to-all-done.2 = bf16[64,3,2048]{2,1,0:T(4,128)(2,1)S(1)} async-done(((bf16[64,3,2048]{2,1,0:T(4,128)(2,1)}), bf16[64,3,2048]{2,1,0:T(4,128)(2,1)S(1)}, u32[]{:S(2)}, u32[]{:S(2)}) %all-to-all-start.2) | async-done | bytes 786464 | tf_op jit(solution)/shard_map/all_to_all | solution.py:77
  408.9 0.7 reshape.90
  409.6 1.7 gather_fusion.2
  411.3 151.5 %reduce-scatter.4.cloned.1.call-done = bf16[128,768]{1,0:T(8,128)(2,1)} async-done(((bf16[2048,768]{1,0:T(8,128)(2,1)}), bf16[128,768]{1,0:T(8,128)(2,1)}) %reduce-scatter.4.cloned.1.call-update) | async-done | bytes 196624
  562.8 1.1 copy.24
  564.0 0.8 copy.22
  564.7 0.8 copy.21
  565.5 0.8 copy.20
  (37 shorter events, 4.7 us)
Async XLA Ops:
  7.2 1.8 copy-start
  9.0 1.7 copy-start.1
  14.7 72.9 %all-to-all-start = ((bf16[64,3,2048]{2,1,0:T(4,128)(2,1)}), bf16[64,3,2048]{2,1,0:T(4,128)(2,1)S(1)}, u32[]{:S(2)}, u32[]{:S(2)}) async-start(bf16[64,3,2048]{2,1,0:T(4,128)(2,1)} %get-tuple-element.27), calls=%async_computation | async-start | bytes 2097152 | tf_op jit(solution)/shard_map/all_to_all | solution.py:46
  35.4 113.0 %all-gather.11.cloned.1.call-start = ((), (), s32[]{:S(2)}) async-start(), calls=%async_computation.6 | async-start | bytes 1114112 | tf_op jit(solution)/shard_map/all_gather | solution.py:60
  36.1 197.4 %all-gather.9.cloned.1.call-start = ((), (), s32[]{:S(2)}) async-start(), calls=%async_computation.5 | async-start | bytes 1114112 | tf_op jit(solution)/shard_map/all_gather | solution.py:61
  87.6 60.0 %all-to-all-start.1 = ((bf16[64,3,2048]{2,1,0:T(4,128)(2,1)}), bf16[64,3,2048]{2,1,0:T(4,128)(2,1)S(1)}, u32[]{:S(2)}, u32[]{:S(2)}) async-start(bf16[64,3,2048]{2,1,0:T(4,128)(2,1)} %get-tuple-element.28), calls=%async_computation.1 | async-start | bytes 2097152 | tf_op jit(solution)/shard_map/all_to_all | solution.py:39
  95.4 234.5 %all-gather.7.cloned.1.call-start = ((), (), s32[]{:S(2)}) async-start(), calls=%async_computation.4 | async-start | bytes 1114112 | tf_op jit(solution)/shard_map/all_gather | solution.py:62
  96.1 466.7 %reduce-scatter.4.cloned.1.call-start = ((), (), s32[]{:S(2)}) async-start(), calls=%async_computation.7 | async-start | bytes 3342336
  235.1 0.7 copy-start.4
  331.5 0.6 copy-start.5
  339.2 1.2 copy-start.3
  339.2 1.2 copy-start.6
  339.2 1.7 copy-start.2
  342.7 66.2 %all-to-all-start.2 = ((bf16[64,3,2048]{2,1,0:T(4,128)(2,1)}), bf16[64,3,2048]{2,1,0:T(4,128)(2,1)S(1)}, u32[]{:S(2)}, u32[]{:S(2)}) async-start(bf16[64,3,2048]{2,1,0:T(4,128)(2,1)} %reshape.89), calls=%async_computation.2 | async-start | bytes 2097152 | tf_op jit(solution)/shard_map/all_to_all | solution.py:77
Sparse Core Ops, SparseCore 0:
  40.6 95.0 all-gather.10
  140.0 93.4 all-gather.8
  237.8 92.0 all-gather.6
  339.3 223.4 reduce-scatter.3
where the time goes:
time: 573 us
  waiting for transfers between devices  484 us (84%)
  starting transfers between devices  42.5 us (7%)
  local copies, waits for them, and re-layouts  18.6 us (3%)
  between operations  14 us (2%)
  matrix products  7.29 us (1%)
  other arithmetic  5.86 us (1%)
    unnamed x5, waiting for transfers between devices  154 us
    all_gather x1, waiting for transfers between devices, shards(): lax.all_gather(down_piece, 'own', axis=0, tiled=True)  93.6 us
    all_gather x1, waiting for transfers between devices, shards(): lax.all_gather(up_piece, 'own', axis=0, tiled=True)  83.5 us
    all_to_all x1, waiting for transfers between devices, shards(): lax.all_to_all(slot_grad.reshape(hot_count, capacity, model_width), 'rep'...  52.2 us
    all_to_all x1, waiting for transfers between devices, shards(): lax.all_to_all(send_dy.reshape(hot_count, capacity, model_width), 'rep',...  50.8 us
    all_to_all x1, waiting for transfers between devices, shards(): lax.all_to_all(send_x.reshape(hot_count, capacity, model_width), 'rep', s...  50.7 us
    all_to_all x1, starting transfers between devices, shards(): lax.all_to_all(send_dy.reshape(hot_count, capacity, model_width), 'rep',...  20.7 us
    all_to_all x1, starting transfers between devices, shards(): lax.all_to_all(slot_grad.reshape(hot_count, capacity, model_width), 'rep'...  13.9 us
  transfers between devices with their start and end apart: 7, of which 6 were waited for; matrix products, arithmetic and copies ran while one was open for 2% of the time, Pallas kernels for 0%

commit v1 on v0

v1 whole, which is shorter than its diff:
```python
import functools

import jax
import jax.numpy as jnp
from jax import lax
from jax.experimental import pallas as pl
from jax.experimental.pallas import tpu as pltpu
from jax.sharding import PartitionSpec as P

MESH = pl.DeviceIdType.MESH
CAP = 3
CORES = 2
X_LO = 2
X_HI = 2


def nn(left, right):
    return lax.dot_general(
        left, right, (((1,), (0,)), ((), ())), preferred_element_type=jnp.float32
    )


def nt(left, right):
    return lax.dot_general(
        left, right, (((1,), (1,)), ((), ())), preferred_element_type=jnp.float32
    )


def tn(left, right):
    return lax.dot_general(
        left, right, (((0,), (0,)), ((), ())), preferred_element_type=jnp.float32
    )


def kernel(
    n_own,
    n_rep,
    src_ref,
    pos_ref,
    tok_ref,
    cot_ref,
    wg_ref,
    wu_ref,
    wd_ref,
    xg_ref,
    gg_ref,
    gu_ref,
    gd_ref,
    send,
    recv,
    weights,
    wide,
    xs,
    dys,
    grads_h,
    hidden_s,
    back,
    returned,
    stage,
    chain,
    cross,
    crossed,
    local_sem,
    a2a_send,
    a2a_recv,
    ret_send,
    ret_recv,
    agx_send,
    agx_recv,
    ag_send,
    ag_recv,
    rs_send,
    rs_recv,
    rsx_send,
    rsx_recv,
):
    n_y = n_own // X_HI
    n_z = n_rep // (X_LO * CORES)
    half = n_y // 2
    rows = n_rep * CAP
    me_o = lax.axis_index("own")
    me_r = lax.axis_index("rep")
    y = me_o // X_HI
    xh = lax.rem(me_o, X_HI)
    xl = me_r // (n_z * CORES)
    z = lax.rem(me_r // CORES, n_z)
    core = lax.rem(me_r, CORES)

    def own_at(dy, h):
        return lax.rem(y + dy + n_y, n_y) * X_HI + h

    right = (own_at(1, xh), me_r)
    left = (own_at(-1, xh), me_r)
    partner = (y * X_HI + (1 - xh), me_r)
    towards = (right, left)

    def rep_at(dz, dxl, dc):
        return (
            lax.rem(xl + dxl, X_LO) * (n_z * CORES)
            + lax.rem(z + dz + n_z, n_z) * CORES
            + lax.rem(core + dc, CORES)
        )

    def each_peer(body):
        def far(k, carry):
            distance = n_z // 2 - (k + 1) // 2
            dz = jnp.where(lax.rem(k, 2) == 0, -distance, distance)
            for dxl in range(X_LO):
                for dc in range(CORES):
                    body(rep_at(dz, dxl, dc))
            return carry

        lax.fori_loop(0, n_z - 1, far, 0)
        for dxl in range(X_LO):
            for dc in range(CORES):
                if dxl or dc:
                    body(rep_at(0, dxl, dc))

    for k, w_ref in enumerate((wg_ref, wu_ref, wd_ref)):
        pltpu.make_async_copy(w_ref.at[0], weights.at[me_o, k], local_sem.at[k]).start()

    barrier = pltpu.get_barrier_semaphore()
    for dev in (right, left, partner):
        pl.semaphore_signal(barrier, inc=1, device_id=dev, device_id_type=MESH)
    each_peer(
        lambda r: pl.semaphore_signal(
            barrier, inc=1, device_id=(me_o, r), device_id_type=MESH
        )
    )

    def fill(s, carry):
        for c in range(CAP):
            row = src_ref[s * CAP + c]
            send[s * 2 * CAP + c] = tok_ref[row]
            send[s * 2 * CAP + CAP + c] = cot_ref[row]
        return carry

    lax.fori_loop(0, n_rep, fill, 0)
    for k, w_ref in enumerate((wg_ref, wu_ref, wd_ref)):
        pltpu.make_async_copy(w_ref.at[0], weights.at[me_o, k], local_sem.at[k]).wait()
    pl.semaphore_wait(barrier, n_rep - 1 + 3)

    def weight_copy(block, dev, s_sem, r_sem):
        return pltpu.make_async_remote_copy(
            src_ref=weights.at[block],
            dst_ref=weights.at[block],
            send_sem=s_sem,
            recv_sem=r_sem,
            device_id=dev,
            device_id_type=MESH,
        )

    partner_copy = weight_copy(me_o, partner, agx_send, agx_recv)
    partner_copy.start()

    def ring_copy(way, s, other):
        h = (1 - xh) if other else xh
        block = own_at(-s if way == 0 else s, h)
        return weight_copy(
            block,
            towards[way],
            ag_send.at[way, s, int(other)],
            ag_recv.at[way, s, int(other)],
        )

    def ring_hops(s):
        if s < half - 1:
            return [(way, s, other) for other in (False, True) for way in (0, 1)]
        return [(0, s, False), (1, s, True)]

    for way in (0, 1):
        if (way, 0, False) in ring_hops(0):
            ring_copy(way, 0, False).start()

    def token_copy(r):
        return pltpu.make_async_remote_copy(
            src_ref=send.at[pl.ds(r * 2 * CAP, 2 * CAP)],
            dst_ref=recv.at[pl.ds(me_r * 2 * CAP, 2 * CAP)],
            send_sem=a2a_send,
            recv_sem=a2a_recv,
            device_id=(me_o, r),
            device_id_type=MESH,
        )

    each_peer(lambda r: token_copy(r).start())
    self_copy = pltpu.make_async_copy(
        send.at[pl.ds(me_r * 2 * CAP, 2 * CAP)],
        recv.at[pl.ds(me_r * 2 * CAP, 2 * CAP)],
        local_sem.at[0],
    )
    self_copy.start()

    partner_copy.wait()
    for way in (0, 1):
        if (way, 0, True) in ring_hops(0):
            ring_copy(way, 0, True).start()
    for s in range(half):
        for way, s_, other in ring_hops(s):
            ring_copy(way, s, other).wait_recv()
            if s + 1 < half and (way, s + 1, other) in ring_hops(s + 1):
                ring_copy(way, s + 1, other).start()

    self_copy.wait()

    def whole(buffer, sem, per_peer):
        view = buffer.at[pl.ds(0, (n_rep - 1) * per_peer)]
        return pltpu.make_async_copy(view, view, sem)

    whole(recv, a2a_recv, 2 * CAP).wait()

    def widen(r, carry):
        block = recv[pl.ds(r * 2 * CAP, 2 * CAP)].astype(jnp.float32)
        at = r * CAP * n_own
        for c in range(CAP):
            wide[0, pl.ds(at + c * n_own, n_own), :] = block[c]
            wide[1, pl.ds(at + c * n_own, n_own), :] = block[CAP + c]
        return carry

    lax.fori_loop(0, n_rep, widen, 0)

    gate = jnp.zeros((rows, wg_ref.shape[2]), jnp.float32)
    up = jnp.zeros_like(gate)
    grad_back = jnp.zeros_like(gate)
    for p in range(n_y):
        pair = [
            jnp.concatenate(
                [
                    wide[i, pl.ds(X_HI * p + h, rows, stride=n_own), :].astype(jnp.bfloat16)
                    for h in range(X_HI)
                ],
                axis=1,
            )
            for i in range(2)
        ]
        xs[p] = pair[0]
        dys[p] = pair[1]
        w_of = [
            jnp.concatenate([weights[X_HI * p + h, k] for h in range(X_HI)], axis=0)
            for k in range(3)
        ]
        gate += nn(pair[0], w_of[0])
        up += nn(pair[0], w_of[1])
        grad_back += nn(pair[1], w_of[2])

    sg = jax.nn.sigmoid(gate)
    silu = gate * sg
    hidden_s[...] = (silu * up).astype(jnp.bfloat16)
    hw = gate.shape[1]
    grads_h[:, :hw] = (grad_back * up * sg * (1.0 + gate * (1.0 - sg))).astype(jnp.bfloat16)
    grads_h[:, hw:] = (grad_back * silu).astype(jnp.bfloat16)

    for p in range(n_y):
        for h in range(X_HI):
            j = X_HI * p + h
            part = nt(grads_h[:, :hw], weights[j, 0]) + nt(grads_h[:, hw:], weights[j, 1])
            wide[0, pl.ds(j, rows, stride=n_own), :] = part

    def narrow(r, carry):
        for c in range(CAP):
            at = (r * CAP + c) * n_own
            back[r * CAP + c] = wide[0, pl.ds(at, n_own), :].astype(jnp.bfloat16)
        return carry

    lax.fori_loop(0, n_rep, narrow, 0)

    def return_copy(r):
        return pltpu.make_async_remote_copy(
            src_ref=back.at[pl.ds(r * CAP, CAP)],
            dst_ref=returned.at[pl.ds(me_r * CAP, CAP)],
            send_sem=ret_send,
            recv_sem=ret_recv,
            device_id=(me_o, r),
            device_id_type=MESH,
        )

    each_peer(lambda r: return_copy(r).start())
    back_copy = pltpu.make_async_copy(
        back.at[pl.ds(me_r * CAP, CAP)],
        returned.at[pl.ds(me_r * CAP, CAP)],
        local_sem.at[0],
    )
    back_copy.start()

    def terms(dy):
        p = lax.rem(y + dy + n_y, n_y)
        both = tn(xs[p], grads_h[...])
        down = tn(dys[p], hidden_s[...])
        size = both.shape[0] // X_HI
        out = []
        for h in range(X_HI):
            piece = slice(h * size, (h + 1) * size)
            out.append([both[piece, :hw], both[piece, hw:], down[piece]])
        return out

    def sum_copy(way, s, h):
        return pltpu.make_async_remote_copy(
            src_ref=stage.at[way, s, h],
            dst_ref=chain.at[way, s, h],
            send_sem=rs_send.at[way, s, h],
            recv_sem=rs_recv.at[way, s, h],
            device_id=towards[way],
            device_id_type=MESH,
        )

    def columns(way, s):
        return range(X_HI) if s > 0 else (way,)

    for s in range(half):
        shared = terms(half) if s == 0 else None
        for way in (0, 1):
            distance = half - s
            local = shared or terms(distance if way == 0 else -distance)
            for h in columns(way, s):
                arrived = s > 0 and h in columns(way, s - 1)
                if arrived:
                    sum_copy(way, s - 1, h).wait_recv()
                for k in range(3):
                    value = local[h][k].astype(jnp.bfloat16)
                    if arrived:
                        value = (
                            value.astype(jnp.float32)
                            + chain[way, s - 1, h, k].astype(jnp.float32)
                        ).astype(jnp.bfloat16)
                    stage[way, s, h, k] = value
                sum_copy(way, s, h).start()

    local = terms(0)
    for h in range(X_HI):
        for k in range(3):
            wide[1, pl.ds((h * 3 + k) * 2 * local[h][k].shape[0], 2 * local[h][k].shape[0]), :] = (
                jnp.concatenate([local[h][k][:, :128], local[h][k][:, 128:]], axis=0)
                .astype(jnp.bfloat16)
                .astype(jnp.float32)
            )
    size = wg_ref.shape[1]

    def summed(h, k):
        at = (h * 3 + k) * 2 * size
        low = wide[1, pl.ds(at, size), :]
        high = wide[1, pl.ds(at + size, size), :]
        total = jnp.concatenate([low, high], axis=1)
        for way in (0, 1):
            total += chain[way, half - 1, h, k].astype(jnp.float32)
        return total

    for h in range(X_HI):
        for way in (0, 1):
            if h in columns(way, half - 1):
                sum_copy(way, half - 1, h).wait_recv()

    for k in range(3):
        cross[k] = jnp.where(xh == 0, summed(1, k), summed(0, k)).astype(jnp.bfloat16)
    cross_copy = pltpu.make_async_remote_copy(
        src_ref=cross,
        dst_ref=crossed,
        send_sem=rsx_send,
        recv_sem=rsx_recv,
        device_id=partner,
        device_id_type=MESH,
    )
    cross_copy.start()

    back_copy.wait()
    whole(returned, ret_recv, CAP).wait()

    def pick(t, carry):
        xg_ref[t] = returned[pos_ref[t]]
        return carry

    lax.fori_loop(0, xg_ref.shape[0], pick, 0)

    cross_copy.wait()
    for k, out in enumerate((gg_ref, gu_ref, gd_ref)):
        out[0] = jnp.where(xh == 0, summed(0, k), summed(1, k)) + crossed[k].astype(jnp.float32)

    whole(send, a2a_send, 2 * CAP).wait()
    whole(back, ret_send, CAP).wait()
    for s in range(half):
        for way, s_, other in ring_hops(s):
            ring_copy(way, s, other).wait_send()
        for way in (0, 1):
            for h in columns(way, s):
                sum_copy(way, s, h).wait_send()


def shards(n_own, n_rep, tokens, cotangent, route, host, w_gate, w_up, w_down_t):
    tok_rows, width = tokens.shape
    hw = w_gate.shape[2]
    piece = w_gate.shape[1]
    lanes = width // n_own
    rows = n_rep * CAP
    labels = lax.broadcasted_iota(jnp.int32, (tok_rows, n_rep), 1)
    target = jnp.sum(jnp.where(route == labels, host[None, :], 0), axis=1)
    earlier = lax.broadcasted_iota(jnp.int32, (tok_rows, tok_rows), 1) < lax.broadcasted_iota(
        jnp.int32, (tok_rows, tok_rows), 0
    )
    arrival = jnp.sum(
        jnp.where((target[:, None] == target[None, :]) & earlier, 1, 0), axis=1
    )
    position = target * CAP + arrival
    slot_ids = lax.broadcasted_iota(jnp.int32, (rows, tok_rows), 0)
    token_ids = lax.broadcasted_iota(jnp.int32, (rows, tok_rows), 1)
    source = tok_rows + jnp.sum(
        jnp.where(slot_ids == position[None, :], token_ids - tok_rows, 0), axis=1
    )
    tok = jnp.pad(tokens.reshape(tok_rows, n_own, lanes), ((0, 1), (0, 0), (0, 0)))
    cot = jnp.pad(cotangent.reshape(tok_rows, n_own, lanes), ((0, 1), (0, 0), (0, 0)))

    bf16, f32 = jnp.bfloat16, jnp.float32
    half = n_own // X_HI // 2
    vmem = pl.BlockSpec(memory_space=pltpu.VMEM)
    smem = pl.BlockSpec(memory_space=pltpu.SMEM)
    dma = pltpu.SemaphoreType.DMA
    x_rows, gate, up, down = pl.pallas_call(
        functools.partial(kernel, n_own, n_rep),
        out_shape=(
            jax.ShapeDtypeStruct((tok_rows, n_own, lanes), bf16),
            jax.ShapeDtypeStruct((1, piece, hw), f32),
            jax.ShapeDtypeStruct((1, piece, hw), f32),
            jax.ShapeDtypeStruct((1, piece, hw), f32),
        ),
        in_specs=[smem, smem] + [vmem] * 5,
        out_specs=(vmem,) * 4,
        scratch_shapes=[
            pltpu.VMEM((2 * rows, n_own, lanes), bf16),
            pltpu.VMEM((2 * rows, n_own, lanes), bf16),
            pltpu.VMEM((n_own, 3, piece, hw), bf16),
            pltpu.VMEM((2, max(rows * n_own, 12 * piece), lanes), f32),
            pltpu.VMEM((n_own // X_HI, rows, X_HI * lanes), bf16),
            pltpu.VMEM((n_own // X_HI, rows, X_HI * lanes), bf16),
            pltpu.VMEM((rows, 2 * hw), bf16),
            pltpu.VMEM((rows, hw), bf16),
            pltpu.VMEM((rows, n_own, lanes), bf16),
            pltpu.VMEM((rows, n_own, lanes), bf16),
            pltpu.VMEM((2, half, X_HI, 3, piece, hw), bf16),
            pltpu.VMEM((2, half, X_HI, 3, piece, hw), bf16),
            pltpu.VMEM((3, piece, hw), bf16),
            pltpu.VMEM((3, piece, hw), bf16),
            dma((3,)),
            dma,
            dma,
            dma,
            dma,
            dma,
            dma,
            dma((2, half, 2)),
            dma((2, half, 2)),
            dma((2, half, 2)),
            dma((2, half, 2)),
            dma,
            dma,
        ],
        compiler_params=pltpu.CompilerParams(collective_id=0, has_side_effects=True),
    )(source, position, tok, cot, w_gate, w_up, w_down_t)
    return (x_rows.reshape(tok_rows, width), gate, up, down)


def solution(mesh):
    body = functools.partial(shards, mesh.shape["own"], mesh.shape["rep"])
    return jax.shard_map(
        body,
        mesh=mesh,
        in_specs=(
            P(("own", "rep"), None),
            P(("own", "rep"), None),
            P(("own", "rep"), None),
            P(),
            P("rep", "own", None),
            P("rep", "own", None),
            P("rep", "own", None),
        ),
        out_specs=(
            P(("own", "rep"), None),
            P("rep", "own", None),
            P("rep", "own", None),
            P("rep", "own", None),
        ),
        check_vma=False,
    )
```

time: 573 us -> 151 us (0.26)
  the two profiles are of different devices: /device:TPU:16 before, /device:TPU:64 now
where the time goes in v1:
time: 151 us; the launch traced here: 150 us
  Pallas kernels  140 us (93%)
  local copies, waits for them, and re-layouts  9 us (6%)
    pallas_call x1, Pallas kernels, shards(): pl.pallas_call(functools.partial(kernel, n_own, n_rep), out_shape=(jax.Sh...  140 us
    unnamed x20, local copies, waits for them, and re-layouts  7.24 us

profile of v1, /device:TPU:64, one launch (start us, length us, event | category | flops | bytes accessed | tf_op | source)
XLA Modules:
  0.0 150.4 jit_solution(11421262347388609016)
XLA Ops:
  0.6 0.0 copy-start.5
  0.6 0.0 copy-start.6
  0.7 0.6 copy-done.5
  1.3 0.0 copy-done.6
  1.3 0.1 select_reduce_fusion.2
  1.4 0.2 select_reduce_fusion.1
  1.6 0.0 copy-start.4
  1.6 0.5 copy-done.4
  2.1 0.1 select_reduce_fusion
  2.2 0.6 broadcast_add_fusion.src_ref
  2.8 1.1 copy.11
  3.9 0.0 copy-start
  4.0 0.9 pad.7.tok_ref
  4.8 0.2 copy-done
  5.1 0.1 copy.12
  5.2 0.9 pad.8.cot_ref
  6.1 139.7 %shard_map.102 = (bf16[128,16,128]{2,1,0:T(8,128)(2,1)}, f32[1,128,256]{2,1,0:T(8,128)}, f32[1,128,256]{2,1,0:T(8,128)}, f32[1,128,256]{2,1,0:T(8,128)}) custom-call(s32[192]{0:T(256)} %broadcast_add_fusion.src_ref, s32[128]{0:T(128)} %copy-done.4, bf16[129,16,128]{2,1,0:T(8,128)(2,1)} %pad.7.tok_ref, bf16[129,16,128]{2,1,0:T(8,128)(2,1)} %pad.8.cot_ref, ...), custom_call_target="tpu_custom_call" | custom-call | tf_op jit(solution)/shard_map/pallas_call | solution.py:414
  145.8 0.0 copy-start.3
  145.8 2.0 %copy.15 = bf16[16,8,16,128]{3,1,2,0:T(8,128)(2,1)} copy(bf16[16,8,16,128]{3,2,1,0:T(8,128)(2,1)} %bitcast.14) | data formatting | bytes 1048576
  147.8 0.0 copy-done.3
  147.8 0.0 copy-start.2
  147.8 0.7 copy.19
  148.5 0.3 copy-done.2
  148.8 0.0 copy-start.1
  148.8 0.7 copy.20
  149.4 0.3 copy-done.1
  149.7 0.7 copy.21
  (1 shorter events, 0.0 us)
Async XLA Ops:
  0.6 0.7 copy-start.5
  0.6 0.7 copy-start.6
  1.6 0.5 copy-start.4
  3.9 1.1 copy-start
  145.8 2.0 %copy-start.3 = (f32[1,128,256]{2,1,0:T(8,128)S(1)}, f32[1,128,256]{2,1,0:T(8,128)}, u32[]{:S(2)}) copy-start(f32[1,128,256]{2,1,0:T(8,128)} %get-tuple-element.19) | copy-start | bytes 393220
  147.8 1.0 copy-start.2
  148.8 1.0 copy-start.1

commit v2 on v1

v2 whole, which is shorter than its diff:
```python
import functools

import jax
import jax.numpy as jnp
from jax import lax
from jax.experimental import pallas as pl
from jax.experimental.pallas import tpu as pltpu
from jax.sharding import PartitionSpec as P

MESH = pl.DeviceIdType.MESH
CAP = 3
CORES = 2
X_LO = 2
X_HI = 2


def nn(left, right):
    return lax.dot_general(
        left, right, (((1,), (0,)), ((), ())), preferred_element_type=jnp.float32
    )


def nt(left, right):
    return lax.dot_general(
        left, right, (((1,), (1,)), ((), ())), preferred_element_type=jnp.float32
    )


def tn(left, right):
    return lax.dot_general(
        left, right, (((0,), (0,)), ((), ())), preferred_element_type=jnp.float32
    )


def kernel(
    n_own,
    n_rep,
    src_ref,
    pos_ref,
    tok_ref,
    cot_ref,
    wg_ref,
    wu_ref,
    wd_ref,
    xg_ref,
    sums_ref,
    tok_in,
    x_of,
    dy_of,
    send,
    recv,
    weights,
    wide,
    xs,
    dys,
    grads_h,
    hidden_s,
    back,
    returned,
    stage,
    chain,
    total,
    cross,
    crossed,
    relay_rows,
    relay_back,
    local_sem,
    ready,
    relay_in,
    relay_out,
    relay_back_in,
    relay_back_out,
    a2a_send,
    a2a_recv,
    ret_send,
    ret_recv,
    agx_send,
    agx_recv,
    ag_send,
    ag_recv,
    rs_send,
    rs_recv,
    rsx_send,
    rsx_recv,
):
    n_y = n_own // X_HI
    n_z = n_rep // (X_LO * CORES)
    half = n_y // 2
    plane = X_LO * CORES
    far = n_z // 2
    quarter = n_z // 4
    group = n_rep // 2
    rows = group * CAP
    hw = wg_ref.shape[2]
    toks = tok_ref.shape[0]
    lanes = tok_ref.shape[1] // n_own
    me_o = lax.axis_index("own")
    me_r = lax.axis_index("rep")
    y = me_o // X_HI
    xh = lax.rem(me_o, X_HI)
    xl = me_r // (n_z * CORES)
    z = lax.rem(me_r // CORES, n_z)
    core = lax.rem(me_r, CORES)

    def own_at(dy, h):
        return lax.rem(y + dy + n_y, n_y) * X_HI + h

    right = (own_at(1, xh), me_r)
    left = (own_at(-1, xh), me_r)
    partner = (y * X_HI + (1 - xh), me_r)
    towards = (right, left)

    def rep_at(dz, dxl, dc):
        return (
            lax.rem(xl + dxl, X_LO) * (n_z * CORES)
            + lax.rem(z + dz + n_z, n_z) * CORES
            + lax.rem(core + dc, CORES)
        )

    def signal(sem, dev):
        pl.semaphore_signal(sem, inc=1, device_id=dev, device_id_type=MESH)

    in_plane = [(dxl, dc) for dxl in range(X_LO) for dc in range(CORES)]
    ahead = (me_o, rep_at(1, 0, 0))
    behind = (me_o, rep_at(-1, 0, 0))
    barrier = pltpu.get_barrier_semaphore()
    for dev in (right, left, partner, ahead, behind):
        signal(barrier, dev)
    for dxl, dc in in_plane[1:]:
        signal(barrier, (me_o, rep_at(0, dxl, dc)))

    loads = [
        pltpu.make_async_copy(ref, tok_in.at[i], local_sem.at[3 + i])
        for i, ref in enumerate((tok_ref, cot_ref))
    ] + [
        pltpu.make_async_copy(w_ref.at[0], weights.at[me_o, k], local_sem.at[k])
        for k, w_ref in enumerate((wg_ref, wu_ref, wd_ref))
    ]
    for copy in loads:
        copy.start()

    for i in range(2):
        loads[i].wait()
        for j in range(n_own):
            wide[i, pl.ds(j, toks, stride=n_own), :] = tok_in[
                i, :, j * lanes : (j + 1) * lanes
            ].astype(jnp.float32)

    def by_token(t, carry):
        at = pl.ds(pl.multiple_of(t * n_own, n_own), n_own)
        x_of[t] = wide[0, at, :].astype(jnp.bfloat16)
        dy_of[t] = wide[1, at, :].astype(jnp.bfloat16)
        return carry

    lax.fori_loop(0, toks, by_token, 0, unroll=4)
    for rows_of in (x_of, dy_of):
        rows_of[toks] = jnp.zeros((n_own, lanes), jnp.bfloat16)

    def fill(s, carry):
        for c in range(CAP):
            row = src_ref[s * CAP + c]
            send[s * 2 * CAP + c] = x_of[row]
            send[s * 2 * CAP + CAP + c] = dy_of[row]
        return carry

    lax.fori_loop(0, n_rep, fill, 0)
    for copy in loads[2:]:
        copy.wait()
    pl.semaphore_wait(barrier, 5 + plane - 1)

    signal(ready.at[0, 0], ahead)
    signal(ready.at[1, 0], behind)

    def weight_copy(block, dev, s_sem, r_sem):
        return pltpu.make_async_remote_copy(
            src_ref=weights.at[block],
            dst_ref=weights.at[block],
            send_sem=s_sem,
            recv_sem=r_sem,
            device_id=dev,
            device_id_type=MESH,
        )

    partner_copy = weight_copy(me_o, partner, agx_send, agx_recv)
    partner_copy.start()

    def ring_copy(way, s, other):
        h = (1 - xh) if other else xh
        block = own_at(-s if way == 0 else s, h)
        return weight_copy(
            block,
            towards[way],
            ag_send.at[way, s, int(other)],
            ag_recv.at[way, s, int(other)],
        )

    def ring_hops(s):
        if s < half - 1:
            return [(way, s, other) for other in (False, True) for way in (0, 1)]
        return [(0, s, False), (1, s, True)]

    for way in (0, 1):
        if (way, 0, False) in ring_hops(0):
            ring_copy(way, 0, False).start()

    def send_plane(dz, at, members):
        for dxl, dc in members:
            r = rep_at(dz, dxl, dc)
            place = at * plane + dxl * CORES + dc
            pltpu.make_async_remote_copy(
                src_ref=send.at[pl.ds(r * 2 * CAP, 2 * CAP)],
                dst_ref=recv.at[pl.ds(place * 2 * CAP, 2 * CAP)],
                send_sem=a2a_send,
                recv_sem=a2a_recv.at[at // far],
                device_id=(me_o, r),
                device_id_type=MESH,
            ).start()

    send_plane(0, 0, in_plane[1:])
    self_copy = pltpu.make_async_copy(
        send.at[pl.ds(me_r * 2 * CAP, 2 * CAP)],
        recv.at[pl.ds(0, 2 * CAP)],
        local_sem.at[0],
    )
    self_copy.start()

    def send_both(d, forward):
        for way, ahead_of in enumerate((ahead, behind)):
            pl.semaphore_wait(ready.at[way, d - 1], 1)
            if forward:
                signal(ready.at[way, d], ahead_of)
        send_plane(d, 2 * d, in_plane)
        send_plane(-d, 2 * d - 1, in_plane)

    def send_planes(first, last):
        def one(d, carry):
            send_both(d, True)
            return carry

        lax.fori_loop(first, min(last + 1, far - 1), one, 0)
        if last == far - 1:
            send_both(last, False)

    ways = [(0, quarter), (1, -quarter)]
    crossing = [(way, dz, dxl) for way, dz in ways for dxl in range(X_LO)]

    def via(src, dst, s_sem, r_sem, dz):
        pltpu.make_async_remote_copy(
            src_ref=src,
            dst_ref=dst,
            send_sem=s_sem,
            recv_sem=r_sem,
            device_id=(me_o, rep_at(dz, 0, 0)),
            device_id_type=MESH,
        ).start()

    send_planes(1, quarter)
    for way, dz, dxl in crossing:
        r = rep_at(far, dxl, way)
        via(
            send.at[pl.ds(r * 2 * CAP, 2 * CAP)],
            relay_rows.at[pl.ds((way * X_LO + dxl) * 2 * CAP, 2 * CAP)],
            a2a_send,
            relay_in,
            dz,
        )
    if quarter < far - 1:
        send_planes(quarter + 1, far - 1)

    def whole(buffer, sem, count):
        view = buffer.at[pl.ds(0, count)]
        return pltpu.make_async_copy(view, view, sem)

    def pass_rows():
        whole(relay_rows, relay_in, len(crossing) * 2 * CAP).wait()
        for way, dz, dxl in crossing:
            place = (n_z - 1) * plane + dxl * CORES + way
            pltpu.make_async_remote_copy(
                src_ref=relay_rows.at[pl.ds((way * X_LO + dxl) * 2 * CAP, 2 * CAP)],
                dst_ref=recv.at[pl.ds(place * 2 * CAP, 2 * CAP)],
                send_sem=relay_out,
                recv_sem=a2a_recv.at[1],
                device_id=(me_o, rep_at(dz, dxl, way)),
                device_id_type=MESH,
            ).start()

    def pass_back():
        whole(relay_back, relay_back_in, len(crossing) * CAP).wait()
        for way, dz, dxl in crossing:
            pltpu.make_async_remote_copy(
                src_ref=relay_back.at[pl.ds((way * X_LO + dxl) * CAP, CAP)],
                dst_ref=returned.at[pl.ds(rep_at(-dz, 0, 0) * CAP, CAP)],
                send_sem=relay_back_out,
                recv_sem=ret_recv,
                device_id=(me_o, rep_at(dz, dxl, way)),
                device_id_type=MESH,
            ).start()

    partner_copy.wait()
    for way in (0, 1):
        if (way, 0, True) in ring_hops(0):
            ring_copy(way, 0, True).start()
    for s in range(half):
        for way, s_, other in ring_hops(s):
            ring_copy(way, s, other).wait_recv()
            if s + 1 < half and (way, s + 1, other) in ring_hops(s + 1):
                ring_copy(way, s + 1, other).start()
        if s == half // 2 - 1:
            pass_rows()

    def forward(g):
        def widen(r, carry):
            block = recv[pl.ds((g * group + r) * 2 * CAP, 2 * CAP)].astype(jnp.float32)
            for c in range(CAP):
                at = pl.ds(pl.multiple_of((r * CAP + c) * n_own, n_own), n_own)
                wide[0, at, :] = block[c]
                wide[1, at, :] = block[CAP + c]
            return carry

        lax.fori_loop(0, group, widen, 0)
        mine = pl.ds(g * rows, rows)
        gate = jnp.zeros((rows, hw), jnp.float32)
        up = jnp.zeros_like(gate)
        grad_back = jnp.zeros_like(gate)
        for p in range(n_y):
            pair = []
            for i, kept in enumerate((xs, dys)):
                parts = []
                for h in range(X_HI):
                    j = X_HI * p + h
                    part = wide[i, pl.ds(j, rows, stride=n_own), :].astype(jnp.bfloat16)
                    kept[j, mine, :] = part
                    parts.append(part)
                pair.append(jnp.concatenate(parts, axis=1))
            w_of = [
                jnp.concatenate([weights[X_HI * p + h, k] for h in range(X_HI)], axis=0)
                for k in range(3)
            ]
            gate += nn(pair[0], w_of[0])
            up += nn(pair[0], w_of[1])
            grad_back += nn(pair[1], w_of[2])
        sg = jax.nn.sigmoid(gate)
        silu = gate * sg
        hidden_s[mine, :] = (silu * up).astype(jnp.bfloat16)
        grads_h[mine, :hw] = (grad_back * up * sg * (1.0 + gate * (1.0 - sg))).astype(jnp.bfloat16)
        grads_h[mine, hw:] = (grad_back * silu).astype(jnp.bfloat16)

    def give_back(g):
        mine = pl.ds(g * rows, rows)
        for j in range(n_own):
            wide[0, pl.ds(j, rows, stride=n_own), :] = nt(
                grads_h[mine, :hw], weights[j, 0]
            ) + nt(grads_h[mine, hw:], weights[j, 1])

        def narrow(r, carry):
            for c in range(CAP):
                at = pl.ds(pl.multiple_of((r * CAP + c) * n_own, n_own), n_own)
                back[g * rows + r * CAP + c] = wide[0, at, :].astype(jnp.bfloat16)
            return carry

        lax.fori_loop(0, group, narrow, 0)

        def home(at, dz, members):
            for dxl, dc in members:
                place = at * plane + dxl * CORES + dc
                pltpu.make_async_remote_copy(
                    src_ref=back.at[pl.ds(place * CAP, CAP)],
                    dst_ref=returned.at[pl.ds(me_r * CAP, CAP)],
                    send_sem=ret_send,
                    recv_sem=ret_recv,
                    device_id=(me_o, rep_at(dz, dxl, dc)),
                    device_id_type=MESH,
                ).start()

        def homes(at, carry):
            up_z = (at + 1) // 2
            home(at, jnp.where(lax.rem(at, 2) == 1, up_z, -up_z), in_plane)
            return carry

        if g == 0:
            home(0, 0, in_plane[1:])
            lax.fori_loop(1, far, homes, 0)
            return
        for way, dz, dxl in crossing:
            place = (n_z - 1) * plane + dxl * CORES + way
            via(
                back.at[pl.ds(place * CAP, CAP)],
                relay_back.at[pl.ds((way * X_LO + dxl) * CAP, CAP)],
                ret_send,
                relay_back_in,
                dz,
            )
        lax.fori_loop(far, n_z - 1, homes, 0)

    self_copy.wait()
    whole(recv, a2a_recv.at[0], (group - 1) * 2 * CAP).wait()
    forward(0)
    give_back(0)
    back_copy = pltpu.make_async_copy(
        back.at[pl.ds(0, CAP)], returned.at[pl.ds(me_r * CAP, CAP)], local_sem.at[0]
    )
    back_copy.start()
    whole(recv, a2a_recv.at[1], group * 2 * CAP).wait()
    forward(1)

    def terms(dy, column):
        j = own_at(dy, xh if column else 1 - xh)
        both = tn(xs[j], grads_h[...])
        return both[:, :hw], both[:, hw:], tn(dys[j], hidden_s[...])

    def sum_copy(way, s, column):
        return pltpu.make_async_remote_copy(
            src_ref=stage.at[way, s, column],
            dst_ref=chain.at[way, s, column],
            send_sem=rs_send.at[way, s, column],
            recv_sem=rs_recv.at[way, s, column],
            device_id=towards[way],
            device_id_type=MESH,
        )

    def columns(way, s):
        return range(X_HI) if s > 0 else (way,)

    def put_terms(s):
        for column in range(X_HI):
            for way in (0, 1):
                if column in columns(way, s):
                    distance = half - s
                    for k, term in enumerate(terms(distance if way == 0 else -distance, column)):
                        stage[way, s, column, k] = term.astype(jnp.bfloat16)

    put_terms(0)
    for way in (0, 1):
        sum_copy(way, 0, way).start()
    give_back(1)
    for s in range(1, half):
        put_terms(s)
        for column in range(X_HI):
            for way in (0, 1):
                if column in columns(way, s - 1):
                    sum_copy(way, s - 1, column).wait_recv()
                    for k in range(3):
                        stage[way, s, column, k] = (
                            stage[way, s, column, k].astype(jnp.float32)
                            + chain[way, s - 1, column, k].astype(jnp.float32)
                        ).astype(jnp.bfloat16)
                sum_copy(way, s, column).start()
        if s == min(2, half - 1):
            pass_back()
    for column in range(X_HI):
        for k, term in enumerate(terms(0, column)):
            total[column, k] = term.astype(jnp.bfloat16).astype(jnp.float32)

    def summed(column, k):
        return (
            total[column, k]
            + chain[0, half - 1, column, k].astype(jnp.float32)
            + chain[1, half - 1, column, k].astype(jnp.float32)
        )

    for way in (0, 1):
        sum_copy(way, half - 1, 0).wait_recv()
    for k in range(3):
        cross[k] = summed(0, k).astype(jnp.bfloat16)
    cross_copy = pltpu.make_async_remote_copy(
        src_ref=cross,
        dst_ref=crossed,
        send_sem=rsx_send,
        recv_sem=rsx_recv,
        device_id=partner,
        device_id_type=MESH,
    )
    cross_copy.start()
    for way in (0, 1):
        sum_copy(way, half - 1, 1).wait_recv()
    for k in range(3):
        total[1, k] = summed(1, k)

    back_copy.wait()
    whole(returned, ret_recv, (n_rep - 1) * CAP).wait()

    def pick(t, carry):
        xg_ref[t] = returned[pos_ref[t]]
        return carry

    lax.fori_loop(0, toks, pick, 0)

    cross_copy.wait()
    for k in range(3):
        sums_ref[k] = total[1, k] + crossed[k].astype(jnp.float32)

    whole(send, a2a_send, (n_rep - 1) * 2 * CAP).wait()
    whole(back, ret_send, (n_rep - 1) * CAP).wait()
    whole(relay_rows, relay_out, len(crossing) * 2 * CAP).wait()
    whole(relay_back, relay_back_out, len(crossing) * CAP).wait()
    for s in range(half):
        for way, s_, other in ring_hops(s):
            ring_copy(way, s, other).wait_send()
        for way in (0, 1):
            for column in columns(way, s):
                sum_copy(way, s, column).wait_send()


def shards(n_own, n_rep, tokens, cotangent, route, host, w_gate, w_up, w_down_t):
    tok_rows, width = tokens.shape
    hw = w_gate.shape[2]
    piece = w_gate.shape[1]
    lanes = width // n_own
    rows = n_rep * CAP
    labels = lax.broadcasted_iota(jnp.int32, (tok_rows, n_rep), 1)
    target = jnp.sum(jnp.where(route == labels, host[None, :], 0), axis=1)
    earlier = lax.broadcasted_iota(jnp.int32, (tok_rows, tok_rows), 1) < lax.broadcasted_iota(
        jnp.int32, (tok_rows, tok_rows), 0
    )
    arrival = jnp.sum(
        jnp.where((target[:, None] == target[None, :]) & earlier, 1, 0), axis=1
    )
    position = target * CAP + arrival
    slot_ids = lax.broadcasted_iota(jnp.int32, (rows, tok_rows), 0)
    token_ids = lax.broadcasted_iota(jnp.int32, (rows, tok_rows), 1)
    source = tok_rows + jnp.sum(
        jnp.where(slot_ids == position[None, :], token_ids - tok_rows, 0), axis=1
    )
    bf16, f32 = jnp.bfloat16, jnp.float32
    half = n_own // X_HI // 2
    vmem = pl.BlockSpec(memory_space=pltpu.VMEM)
    smem = pl.BlockSpec(memory_space=pltpu.SMEM)
    anywhere = pl.BlockSpec(memory_space=pl.ANY)
    dma = pltpu.SemaphoreType.DMA
    x_rows, sums = pl.pallas_call(
        functools.partial(kernel, n_own, n_rep),
        out_shape=(
            jax.ShapeDtypeStruct((tok_rows, n_own, lanes), bf16),
            jax.ShapeDtypeStruct((3, piece, hw), f32),
        ),
        in_specs=[smem, smem] + [anywhere] * 5,
        out_specs=(vmem,) * 2,
        scratch_shapes=[
            pltpu.VMEM((2, tok_rows, width), bf16),
            pltpu.VMEM((tok_rows + 1, n_own, lanes), bf16),
            pltpu.VMEM((tok_rows + 1, n_own, lanes), bf16),
            pltpu.VMEM((2 * rows, n_own, lanes), bf16),
            pltpu.VMEM((2 * rows, n_own, lanes), bf16),
            pltpu.VMEM((n_own, 3, piece, hw), bf16),
            pltpu.VMEM((2, max(rows // 2, tok_rows) * n_own, lanes), f32),
            pltpu.VMEM((n_own, rows, lanes), bf16),
            pltpu.VMEM((n_own, rows, lanes), bf16),
            pltpu.VMEM((rows, 2 * hw), bf16),
            pltpu.VMEM((rows, hw), bf16),
            pltpu.VMEM((rows, n_own, lanes), bf16),
            pltpu.VMEM((rows, n_own, lanes), bf16),
            pltpu.VMEM((2, half, X_HI, 3, piece, hw), bf16),
            pltpu.VMEM((2, half, X_HI, 3, piece, hw), bf16),
            pltpu.VMEM((X_HI, 3, piece, hw), f32),
            pltpu.VMEM((3, piece, hw), bf16),
            pltpu.VMEM((3, piece, hw), bf16),
            pltpu.VMEM((4 * CAP * X_LO, n_own, lanes), bf16),
            pltpu.VMEM((2 * CAP * X_LO, n_own, lanes), bf16),
            dma((5,)),
            pltpu.SemaphoreType.REGULAR((2, n_rep // (X_LO * CORES) // 2 - 1)),
            dma,
            dma,
            dma,
            dma,
            dma,
            dma((2,)),
            dma,
            dma,
            dma,
            dma,
            dma((2, half, 2)),
            dma((2, half, 2)),
            dma((2, half, 2)),
            dma((2, half, 2)),
            dma,
            dma,
        ],
        compiler_params=pltpu.CompilerParams(collective_id=0, has_side_effects=True),
    )(source, position, tokens, cotangent, w_gate, w_up, w_down_t)
    return (x_rows.reshape(tok_rows, width), sums[0:1], sums[1:2], sums[2:3])


def solution(mesh):
    body = functools.partial(shards, mesh.shape["own"], mesh.shape["rep"])
    return jax.shard_map(
        body,
        mesh=mesh,
        in_specs=(
            P(("own", "rep"), None),
            P(("own", "rep"), None),
            P(("own", "rep"), None),
            P(),
            P("rep", "own", None),
            P("rep", "own", None),
            P("rep", "own", None),
        ),
        out_specs=(
            P(("own", "rep"), None),
            P("rep", "own", None),
            P("rep", "own", None),
            P("rep", "own", None),
        ),
        check_vma=False,
    )
```

time: 151 us -> 138 us (0.914)
  the two profiles are of different devices: /device:TPU:64 before, /device:TPU:128 now
where the time goes in v2:
time: 138 us; the launch traced here: 137 us
  Pallas kernels  132 us (96%)
  local copies, waits for them, and re-layouts  3.94 us (3%)
    pallas_call x1, Pallas kernels, shards(): pl.pallas_call(functools.partial(kernel, n_own, n_rep), out_shape=(jax.Sh...  132 us
    unnamed x9, local copies, waits for them, and re-layouts  3.19 us

profile of v2, /device:TPU:128, one launch (start us, length us, event | category | flops | bytes accessed | tf_op | source)
XLA Modules:
  0.0 137.3 jit_solution(18310840439673900333)
XLA Ops:
  0.6 0.0 copy-start.2
  0.6 0.0 copy-start.3
  0.7 0.6 copy-done.2
  1.3 0.0 copy-done.3
  1.3 0.1 select_reduce_fusion.2
  1.4 0.2 select_reduce_fusion.1
  1.6 0.0 copy-start.1
  1.6 0.5 copy-done.1
  2.1 0.1 select_reduce_fusion
  2.2 0.6 broadcast_add_fusion.src_ref
  2.8 131.7 %shard_map.102 = (bf16[128,16,128]{2,1,0:T(8,128)(2,1)}, f32[3,128,256]{2,1,0:T(8,128)}) custom-call(s32[192]{0:T(256)} %broadcast_add_fusion.src_ref, s32[128]{0:T(128)} %copy-done.1, bf16[128,2048]{1,0:T(8,128)(2,1)} %tok_ref.1, bf16[128,2048]{1,0:T(8,128)(2,1)} %cot_ref.1, bf16[1,128,256]{2,1,0:T(8,128)(2,1)} %wg_ref.1, bf16[1,128,256]{2,1,0:T(8,128)(2,1)} %wu_ref.1, ...), custom_call_target="tpu_custom_call" | custom-call | tf_op jit(solution)/shard_map/pallas_call | solution.py:530
  134.5 0.0 copy-start
  134.5 2.0 %copy.13 = bf16[16,8,16,128]{3,1,2,0:T(8,128)(2,1)} copy(bf16[16,8,16,128]{3,2,1,0:T(8,128)(2,1)} %bitcast.6) | data formatting | bytes 1048576
  136.5 0.0 copy-done
  136.5 0.8 fusion.1
  (1 shorter events, 0.0 us)
Async XLA Ops:
  0.6 0.7 copy-start.2
  0.6 0.7 copy-start.3
  1.6 0.5 copy-start.1
  134.5 2.0 %copy-start = (f32[3,128,256]{2,1,0:T(8,128)S(1)}, f32[3,128,256]{2,1,0:T(8,128)}, u32[]{:S(2)}) copy-start(f32[3,128,256]{2,1,0:T(8,128)} %get-tuple-element.7) | copy-start | bytes 1179652

commit v3 on v2

--- a/solution.py
+++ b/solution.py
@@ -35,8 +35,8 @@
 def kernel(
     n_own,
     n_rep,
-    src_ref,
-    pos_ref,
+    route_ref,
+    host_ref,
     tok_ref,
     cot_ref,
     wg_ref,
@@ -44,6 +44,10 @@
     wd_ref,
     xg_ref,
     sums_ref,
+    route_in,
+    host_in,
+    table,
+    index,
     tok_in,
     x_of,
     dy_of,
@@ -129,6 +133,10 @@
     for dxl, dc in in_plane[1:]:
         signal(barrier, (me_o, rep_at(0, dxl, dc)))
 
+    names = [
+        pltpu.make_async_copy(route_ref, route_in, local_sem.at[5]),
+        pltpu.make_async_copy(host_ref, host_in, local_sem.at[6]),
+    ]
     loads = [
         pltpu.make_async_copy(ref, tok_in.at[i], local_sem.at[3 + i])
         for i, ref in enumerate((tok_ref, cot_ref))
@@ -136,8 +144,36 @@
         pltpu.make_async_copy(w_ref.at[0], weights.at[me_o, k], local_sem.at[k])
         for k, w_ref in enumerate((wg_ref, wu_ref, wd_ref))
     ]
-    for copy in loads:
+    for copy in names + loads:
         copy.start()
+
+    for copy in names:
+        copy.wait()
+    def across(shape, axis):
+        return lax.broadcasted_iota(jnp.int32, shape, axis)
+
+    def turned(row, size):
+        eye = across((size, row.shape[1]), 0) == across((size, row.shape[1]), 1)
+        return jnp.sum(jnp.where(eye, row, 0), axis=1, keepdims=True)
+
+    route_row = route_in[...]
+    host_col = turned(host_in[...], n_rep)
+    named = across((n_rep, toks), 0) == route_row
+    target_row = jnp.sum(jnp.where(named, host_col, 0), axis=0, keepdims=True)
+    square = (toks, toks)
+    same = (turned(target_row, toks) == target_row) & (across(square, 0) < across(square, 1))
+    arrival_row = jnp.sum(jnp.where(same, 1, 0), axis=0, keepdims=True)
+    position_row = target_row * CAP + arrival_row
+    slots = index.shape[1]
+    spread = (toks, slots)
+    holds = turned(position_row, toks) == across(spread, 1)
+    source_row = toks + jnp.sum(
+        jnp.where(holds, across(spread, 0) - toks, 0), axis=0, keepdims=True
+    )
+    table[0:1, :] = source_row
+    table[1:2, 0:toks] = position_row
+    to_scalars = pltpu.make_async_copy(table, index, local_sem.at[5])
+    to_scalars.start()
 
     for i in range(2):
         loads[i].wait()
@@ -156,14 +192,21 @@
     for rows_of in (x_of, dy_of):
         rows_of[toks] = jnp.zeros((n_own, lanes), jnp.bfloat16)
 
-    def fill(s, carry):
-        for c in range(CAP):
-            row = src_ref[s * CAP + c]
-            send[s * 2 * CAP + c] = x_of[row]
-            send[s * 2 * CAP + CAP + c] = dy_of[row]
-        return carry
-
-    lax.fori_loop(0, n_rep, fill, 0)
+    def fill_plane(dz):
+        for dxl, dc in in_plane:
+            r = rep_at(dz, dxl, dc)
+            for c in range(CAP):
+                row = jnp.clip(index[0, r * CAP + c], 0, toks)
+                send[r * 2 * CAP + c] = x_of[row]
+                send[r * 2 * CAP + CAP + c] = dy_of[row]
+
+    def fill_both(d):
+        fill_plane(d)
+        fill_plane(-d)
+
+    to_scalars.wait()
+    fill_plane(0)
+    fill_both(1)
     for copy in loads[2:]:
         copy.wait()
     pl.semaphore_wait(barrier, 5 + plane - 1)
@@ -231,6 +274,8 @@
                 signal(ready.at[way, d], ahead_of)
         send_plane(d, 2 * d, in_plane)
         send_plane(-d, 2 * d - 1, in_plane)
+        if forward:
+            fill_both(d + 1)
 
     def send_planes(first, last):
         def one(d, carry):
@@ -254,6 +299,7 @@
             device_id_type=MESH,
         ).start()
 
+    fill_plane(far)
     send_planes(1, quarter)
     for way, dz, dxl in crossing:
         r = rep_at(far, dxl, way)
@@ -480,7 +526,7 @@
     whole(returned, ret_recv, (n_rep - 1) * CAP).wait()
 
     def pick(t, carry):
-        xg_ref[t] = returned[pos_ref[t]]
+        xg_ref[t] = returned[jnp.clip(index[1, t], 0, n_rep * CAP - 1)]
         return carry
 
     lax.fori_loop(0, toks, pick, 0)
@@ -507,24 +553,10 @@
     piece = w_gate.shape[1]
     lanes = width // n_own
     rows = n_rep * CAP
-    labels = lax.broadcasted_iota(jnp.int32, (tok_rows, n_rep), 1)
-    target = jnp.sum(jnp.where(route == labels, host[None, :], 0), axis=1)
-    earlier = lax.broadcasted_iota(jnp.int32, (tok_rows, tok_rows), 1) < lax.broadcasted_iota(
-        jnp.int32, (tok_rows, tok_rows), 0
-    )
-    arrival = jnp.sum(
-        jnp.where((target[:, None] == target[None, :]) & earlier, 1, 0), axis=1
-    )
-    position = target * CAP + arrival
-    slot_ids = lax.broadcasted_iota(jnp.int32, (rows, tok_rows), 0)
-    token_ids = lax.broadcasted_iota(jnp.int32, (rows, tok_rows), 1)
-    source = tok_rows + jnp.sum(
-        jnp.where(slot_ids == position[None, :], token_ids - tok_rows, 0), axis=1
-    )
     bf16, f32 = jnp.bfloat16, jnp.float32
     half = n_own // X_HI // 2
     vmem = pl.BlockSpec(memory_space=pltpu.VMEM)
-    smem = pl.BlockSpec(memory_space=pltpu.SMEM)
+    table = (2, -(-max(rows, tok_rows) // 128) * 128)
     anywhere = pl.BlockSpec(memory_space=pl.ANY)
     dma = pltpu.SemaphoreType.DMA
     x_rows, sums = pl.pallas_call(
@@ -533,9 +565,13 @@
             jax.ShapeDtypeStruct((tok_rows, n_own, lanes), bf16),
             jax.ShapeDtypeStruct((3, piece, hw), f32),
         ),
-        in_specs=[smem, smem] + [anywhere] * 5,
+        in_specs=[anywhere] * 7,
         out_specs=(vmem,) * 2,
         scratch_shapes=[
+            pltpu.VMEM((1, tok_rows), jnp.int32),
+            pltpu.VMEM((1, n_rep), jnp.int32),
+            pltpu.VMEM(table, jnp.int32),
+            pltpu.SMEM(table, jnp.int32),
             pltpu.VMEM((2, tok_rows, width), bf16),
             pltpu.VMEM((tok_rows + 1, n_own, lanes), bf16),
             pltpu.VMEM((tok_rows + 1, n_own, lanes), bf16),
@@ -556,7 +592,7 @@
             pltpu.VMEM((3, piece, hw), bf16),
             pltpu.VMEM((4 * CAP * X_LO, n_own, lanes), bf16),
             pltpu.VMEM((2 * CAP * X_LO, n_own, lanes), bf16),
-            dma((5,)),
+            dma((7,)),
             pltpu.SemaphoreType.REGULAR((2, n_rep // (X_LO * CORES) // 2 - 1)),
             dma,
             dma,
@@ -576,7 +612,7 @@
             dma,
         ],
         compiler_params=pltpu.CompilerParams(collective_id=0, has_side_effects=True),
-    )(source, position, tokens, cotangent, w_gate, w_up, w_down_t)
+    )(route.reshape(1, tok_rows), host[None], tokens, cotangent, w_gate, w_up, w_down_t)
     return (x_rows.reshape(tok_rows, width), sums[0:1], sums[1:2], sums[2:3])
 
 

time: 138 us -> 134 us (0.971)
  Pallas kernels: 132 us -> 130 us
    unnamed x9 -> x3, local copies, waits for them, and re-layouts: 3.19 us -> 2.03 us
where the time goes in v3:
time: 134 us
  Pallas kernels  130 us (97%)
  local copies, waits for them, and re-layouts  2.78 us (2%)
    pallas_call x1, Pallas kernels, shards(): pl.pallas_call(functools.partial(kernel, n_own, n_rep), out_shape=(jax.Sh...  130 us

profile of v3, /device:TPU:128, one launch (start us, length us, event | category | flops | bytes accessed | tf_op | source)
XLA Modules:
  0.0 133.9 jit_solution(14914547051912592192)
XLA Ops:
  0.6 130.5 %shard_map.102 = (bf16[128,16,128]{2,1,0:T(8,128)(2,1)}, f32[3,128,256]{2,1,0:T(8,128)}) custom-call(s32[1,128]{1,0:T(1,128)} %bitcast.8, s32[1,64]{1,0:T(1,128)} %bitcast.9, bf16[128,2048]{1,0:T(8,128)(2,1)} %tok_ref.1, bf16[128,2048]{1,0:T(8,128)(2,1)} %cot_ref.1, bf16[1,128,256]{2,1,0:T(8,128)(2,1)} %wg_ref.1, bf16[1,128,256]{2,1,0:T(8,128)(2,1)} %wu_ref.1, ...), custom_call_target="tpu_custom_call" | custom-call | tf_op jit(solution)/shard_map/pallas_call | solution.py:562
  131.1 0.0 copy-start
  131.1 2.0 %copy.13 = bf16[16,8,16,128]{3,1,2,0:T(8,128)(2,1)} copy(bf16[16,8,16,128]{3,2,1,0:T(8,128)(2,1)} %bitcast.7) | data formatting | bytes 1048576
  133.1 0.0 copy-done
  133.1 0.8 fusion
Async XLA Ops:
  131.1 2.0 %copy-start = (f32[3,128,256]{2,1,0:T(8,128)S(1)}, f32[3,128,256]{2,1,0:T(8,128)}, u32[]{:S(2)}) copy-start(f32[3,128,256]{2,1,0:T(8,128)} %get-tuple-element.7) | copy-start | bytes 1179652

commit v4 on v3

--- a/solution.py
+++ b/solution.py
@@ -66,6 +66,8 @@
     total,
     cross,
     crossed,
+    early,
+    earlier,
     relay_rows,
     relay_back,
     local_sem,
@@ -86,6 +88,8 @@
     rs_recv,
     rsx_send,
     rsx_recv,
+    first_send,
+    first_recv,
 ):
     n_y = n_own // X_HI
     n_z = n_rep // (X_LO * CORES)
@@ -363,7 +367,7 @@
                 wide[1, at, :] = block[CAP + c]
             return carry
 
-        lax.fori_loop(0, group, widen, 0)
+        lax.fori_loop(0, group, widen, 0, unroll=2)
         mine = pl.ds(g * rows, rows)
         gate = jnp.zeros((rows, hw), jnp.float32)
         up = jnp.zeros_like(gate)
@@ -404,7 +408,7 @@
                 back[g * rows + r * CAP + c] = wide[0, at, :].astype(jnp.bfloat16)
             return carry
 
-        lax.fori_loop(0, group, narrow, 0)
+        lax.fori_loop(0, group, narrow, 0, unroll=2)
 
         def home(at, dz, members):
             for dxl, dc in members:
@@ -454,63 +458,107 @@
         both = tn(xs[j], grads_h[...])
         return both[:, :hw], both[:, hw:], tn(dys[j], hidden_s[...])
 
+    size = wg_ref.shape[1]
+    lead = early.shape[2]
+
+    def bounds(way, s, column):
+        low = 0 if column else lead
+        if s:
+            return low, size
+        middle = (low + size) // 2
+        return ((low, middle), (middle, size))[way]
+
     def sum_copy(way, s, column):
+        low, high = bounds(way, s, column)
+        part = (way, s, column, slice(None), pl.ds(low, high - low))
         return pltpu.make_async_remote_copy(
-            src_ref=stage.at[way, s, column],
-            dst_ref=chain.at[way, s, column],
+            src_ref=stage.at[part],
+            dst_ref=chain.at[part],
             send_sem=rs_send.at[way, s, column],
             recv_sem=rs_recv.at[way, s, column],
             device_id=towards[way],
             device_id_type=MESH,
         )
 
-    def columns(way, s):
-        return range(X_HI) if s > 0 else (way,)
-
-    def put_terms(s):
-        for column in range(X_HI):
-            for way in (0, 1):
-                if column in columns(way, s):
-                    distance = half - s
-                    for k, term in enumerate(terms(distance if way == 0 else -distance, column)):
-                        stage[way, s, column, k] = term.astype(jnp.bfloat16)
-
-    put_terms(0)
-    for way in (0, 1):
-        sum_copy(way, 0, way).start()
+    def first_copy(i):
+        return pltpu.make_async_remote_copy(
+            src_ref=early.at[i],
+            dst_ref=earlier.at[i],
+            send_sem=first_send.at[i],
+            recv_sem=first_recv.at[i],
+            device_id=partner,
+            device_id_type=MESH,
+        )
+
+    def blocks(s):
+        if s == 0:
+            return [(0, half, (0, 1))]
+        if s == half:
+            return [(2 * half - 1, 0, ())]
+        return [(2 * s - 1, half - s, (0,)), (2 * s, s - half, (1,))]
+
+    def put_terms(s, column):
+        for i, dy, sides in blocks(s):
+            for k, term in enumerate(terms(dy, column)):
+                value = term.astype(jnp.bfloat16)
+                if not column:
+                    early[i, k] = value[:lead]
+                for way in sides:
+                    low, high = bounds(way, s, column)
+                    stage[way, s, column, k, low:high] = value[low:high]
+                if not sides:
+                    total[column, k] = value.astype(jnp.float32)
+            if not column:
+                first_copy(i).start()
+
+    def add_to(way, s, column, k, low, high, more):
+        stage[way, s, column, k, low:high] = (
+            stage[way, s, column, k, low:high].astype(jnp.float32) + more.astype(jnp.float32)
+        ).astype(jnp.bfloat16)
+
+    def send_sums(s, column):
+        for i, dy, sides in blocks(s):
+            for way in sides:
+                if column and bounds(way, s, column)[0] == 0:
+                    first_copy(i).wait_recv()
+                    for k in range(3):
+                        add_to(way, s, column, k, 0, lead, earlier[i, k])
+                if s:
+                    sum_copy(way, s - 1, column).wait_recv()
+                    low, high = bounds(way, s - 1, column)
+                    for k in range(3):
+                        add_to(way, s, column, k, low, high, chain[way, s - 1, column, k, low:high])
+                sum_copy(way, s, column).start()
+
+    put_terms(0, 0)
+    send_sums(0, 0)
     give_back(1)
+    put_terms(0, 1)
+    put_terms(1, 0)
+    send_sums(0, 1)
     for s in range(1, half):
-        put_terms(s)
-        for column in range(X_HI):
-            for way in (0, 1):
-                if column in columns(way, s - 1):
-                    sum_copy(way, s - 1, column).wait_recv()
-                    for k in range(3):
-                        stage[way, s, column, k] = (
-                            stage[way, s, column, k].astype(jnp.float32)
-                            + chain[way, s - 1, column, k].astype(jnp.float32)
-                        ).astype(jnp.bfloat16)
-                sum_copy(way, s, column).start()
+        put_terms(s, 1)
+        send_sums(s, 0)
+        put_terms(s + 1, 0)
+        send_sums(s, 1)
         if s == min(2, half - 1):
             pass_back()
-    for column in range(X_HI):
-        for k, term in enumerate(terms(0, column)):
-            total[column, k] = term.astype(jnp.bfloat16).astype(jnp.float32)
-
-    def summed(column, k):
-        return (
-            total[column, k]
-            + chain[0, half - 1, column, k].astype(jnp.float32)
-            + chain[1, half - 1, column, k].astype(jnp.float32)
-        )
+    put_terms(half, 1)
+
+    def summed(column, k, low):
+        value = total[column, k, low:]
+        for way in (0, 1):
+            value += chain[way, half - 1, column, k, low:].astype(jnp.float32)
+        return value
 
     for way in (0, 1):
         sum_copy(way, half - 1, 0).wait_recv()
     for k in range(3):
-        cross[k] = summed(0, k).astype(jnp.bfloat16)
+        cross[k, lead:] = summed(0, k, lead).astype(jnp.bfloat16)
+    later = (slice(None), pl.ds(lead, size - lead))
     cross_copy = pltpu.make_async_remote_copy(
-        src_ref=cross,
-        dst_ref=crossed,
+        src_ref=cross.at[later],
+        dst_ref=crossed.at[later],
         send_sem=rsx_send,
         recv_sem=rsx_recv,
         device_id=partner,
@@ -519,8 +567,10 @@
     cross_copy.start()
     for way in (0, 1):
         sum_copy(way, half - 1, 1).wait_recv()
+    first_copy(2 * half - 1).wait_recv()
     for k in range(3):
-        total[1, k] = summed(1, k)
+        total[1, k] = summed(1, k, 0)
+        sums_ref[k, :lead] = total[1, k, :lead] + earlier[2 * half - 1, k].astype(jnp.float32)
 
     back_copy.wait()
     whole(returned, ret_recv, (n_rep - 1) * CAP).wait()
@@ -529,11 +579,11 @@
         xg_ref[t] = returned[jnp.clip(index[1, t], 0, n_rep * CAP - 1)]
         return carry
 
-    lax.fori_loop(0, toks, pick, 0)
+    lax.fori_loop(0, toks, pick, 0, unroll=8)
 
     cross_copy.wait()
     for k in range(3):
-        sums_ref[k] = total[1, k] + crossed[k].astype(jnp.float32)
+        sums_ref[k, lead:] = total[1, k, lead:] + crossed[k, lead:].astype(jnp.float32)
 
     whole(send, a2a_send, (n_rep - 1) * 2 * CAP).wait()
     whole(back, ret_send, (n_rep - 1) * CAP).wait()
@@ -543,8 +593,10 @@
         for way, s_, other in ring_hops(s):
             ring_copy(way, s, other).wait_send()
         for way in (0, 1):
-            for column in columns(way, s):
+            for column in range(X_HI):
                 sum_copy(way, s, column).wait_send()
+    for i in range(2 * half):
+        first_copy(i).wait_send()
 
 
 def shards(n_own, n_rep, tokens, cotangent, route, host, w_gate, w_up, w_down_t):
@@ -590,6 +642,8 @@
             pltpu.VMEM((X_HI, 3, piece, hw), f32),
             pltpu.VMEM((3, piece, hw), bf16),
             pltpu.VMEM((3, piece, hw), bf16),
+            pltpu.VMEM((n_own // X_HI, 3, piece // 4, hw), bf16),
+            pltpu.VMEM((n_own // X_HI, 3, piece // 4, hw), bf16),
             pltpu.VMEM((4 * CAP * X_LO, n_own, lanes), bf16),
             pltpu.VMEM((2 * CAP * X_LO, n_own, lanes), bf16),
             dma((7,)),
@@ -610,6 +664,8 @@
             dma((2, half, 2)),
             dma,
             dma,
+            dma((n_own // X_HI,)),
+            dma((n_own // X_HI,)),
         ],
         compiler_params=pltpu.CompilerParams(collective_id=0, has_side_effects=True),
     )(route.reshape(1, tok_rows), host[None], tokens, cotangent, w_gate, w_up, w_down_t)

time: 134 us -> 130 us (0.970)
  the two profiles are of different devices: /device:TPU:128 before, /device:TPU:133 now
where the time goes in v4:
time: 130 us
  Pallas kernels  127 us (98%)
  local copies, waits for them, and re-layouts  2.78 us (2%)
    pallas_call x1, Pallas kernels, shards(): pl.pallas_call(functools.partial(kernel, n_own, n_rep), out_shape=(jax.Sh...  127 us

profile of v4, /device:TPU:133, one launch (start us, length us, event | category | flops | bytes accessed | tf_op | source)
XLA Modules:
  0.0 130.0 jit_solution(12251519764947451170)
XLA Ops:
  0.6 126.6 %shard_map.102 = (bf16[128,16,128]{2,1,0:T(8,128)(2,1)}, f32[3,128,256]{2,1,0:T(8,128)}) custom-call(s32[1,128]{1,0:T(1,128)} %bitcast.8, s32[1,64]{1,0:T(1,128)} %bitcast.9, bf16[128,2048]{1,0:T(8,128)(2,1)} %tok_ref.1, bf16[128,2048]{1,0:T(8,128)(2,1)} %cot_ref.1, bf16[1,128,256]{2,1,0:T(8,128)(2,1)} %wg_ref.1, bf16[1,128,256]{2,1,0:T(8,128)(2,1)} %wu_ref.1, ...), custom_call_target="tpu_custom_call" | custom-call | tf_op jit(solution)/shard_map/pallas_call | solution.py:614
  127.3 0.0 copy-start
  127.3 2.0 %copy.13 = bf16[16,8,16,128]{3,1,2,0:T(8,128)(2,1)} copy(bf16[16,8,16,128]{3,2,1,0:T(8,128)(2,1)} %bitcast.7) | data formatting | bytes 1048576
  129.3 0.0 copy-done
  129.3 0.8 fusion
Async XLA Ops:
  127.3 2.0 %copy-start = (f32[3,128,256]{2,1,0:T(8,128)S(1)}, f32[3,128,256]{2,1,0:T(8,128)}, u32[]{:S(2)}) copy-start(f32[3,128,256]{2,1,0:T(8,128)} %get-tuple-element.7) | copy-start | bytes 1179652

commit v5 on v4

--- a/solution.py
+++ b/solution.py
@@ -192,7 +192,7 @@
         dy_of[t] = wide[1, at, :].astype(jnp.bfloat16)
         return carry
 
-    lax.fori_loop(0, toks, by_token, 0, unroll=4)
+    lax.fori_loop(0, toks, by_token, 0, unroll=16)
     for rows_of in (x_of, dy_of):
         rows_of[toks] = jnp.zeros((n_own, lanes), jnp.bfloat16)
 
@@ -576,10 +576,16 @@
     whole(returned, ret_recv, (n_rep - 1) * CAP).wait()
 
     def pick(t, carry):
-        xg_ref[t] = returned[jnp.clip(index[1, t], 0, n_rep * CAP - 1)]
+        at = pl.ds(pl.multiple_of(t * n_own, n_own), n_own)
+        row = returned[jnp.clip(index[1, t], 0, n_rep * CAP - 1)]
+        wide[0, at, :] = row.astype(jnp.float32)
         return carry
 
     lax.fori_loop(0, toks, pick, 0, unroll=8)
+    for j in range(n_own):
+        xg_ref[:, j * lanes : (j + 1) * lanes] = wide[
+            0, pl.ds(j, toks, stride=n_own), :
+        ].astype(jnp.bfloat16)
 
     cross_copy.wait()
     for k in range(3):
@@ -614,7 +620,7 @@
     x_rows, sums = pl.pallas_call(
         functools.partial(kernel, n_own, n_rep),
         out_shape=(
-            jax.ShapeDtypeStruct((tok_rows, n_own, lanes), bf16),
+            jax.ShapeDtypeStruct((tok_rows, width), bf16),
             jax.ShapeDtypeStruct((3, piece, hw), f32),
         ),
         in_specs=[anywhere] * 7,
@@ -669,7 +675,7 @@
         ],
         compiler_params=pltpu.CompilerParams(collective_id=0, has_side_effects=True),
     )(route.reshape(1, tok_rows), host[None], tokens, cotangent, w_gate, w_up, w_down_t)
-    return (x_rows.reshape(tok_rows, width), sums[0:1], sums[1:2], sums[2:3])
+    return (x_rows, sums[0:1], sums[1:2], sums[2:3])
 
 
 def solution(mesh):

time: 130 us -> 131 us (level)
  no operation moved by 1% of the time
where the time goes in v5:
time: 131 us; the launch traced here: 130 us
  Pallas kernels  127 us (97%)
  local copies, waits for them, and re-layouts  2.64 us (2%)
    pallas_call x1, Pallas kernels, shards(): pl.pallas_call(functools.partial(kernel, n_own, n_rep), out_shape=(jax.Sh...  127 us

profile of v5, /device:TPU:133, one launch (start us, length us, event | category | flops | bytes accessed | tf_op | source)
XLA Modules:
  0.0 130.3 jit_solution(8190187328808902508)
XLA Ops:
  0.6 127.0 %shard_map.102 = (bf16[128,2048]{1,0:T(8,128)(2,1)}, f32[3,128,256]{2,1,0:T(8,128)}) custom-call(s32[1,128]{1,0:T(1,128)} %bitcast.2, s32[1,64]{1,0:T(1,128)} %bitcast.3, bf16[128,2048]{1,0:T(8,128)(2,1)} %tok_ref.1, bf16[128,2048]{1,0:T(8,128)(2,1)} %cot_ref.1, bf16[1,128,256]{2,1,0:T(8,128)(2,1)} %wg_ref.1, bf16[1,128,256]{2,1,0:T(8,128)(2,1)} %wu_ref.1, ...), custom_call_target="tpu_custom_call" | custom-call | tf_op jit(solution)/shard_map/pallas_call | solution.py:620
  127.7 0.0 copy-start
  127.7 1.8 %fusion = (f32[1,128,256]{2,1,0:T(8,128)}, f32[1,128,256]{2,1,0:T(8,128)}, f32[1,128,256]{2,1,0:T(8,128)}) fusion(f32[3,128,256]{2,1,0:T(8,128)} %get-tuple-element.7), kind=kLoop, calls=%fused_computation | loop fusion | bytes 786432 | tf_op jit(solution)/shard_map/slice | solution.py:678
  129.5 0.0 copy-done
  129.5 0.8 copy.12
Async XLA Ops:
  127.7 1.9 %copy-start = (bf16[128,2048]{1,0:T(8,128)(2,1)S(1)}, bf16[128,2048]{1,0:T(8,128)(2,1)}, u32[]{:S(2)}) copy-start(bf16[128,2048]{1,0:T(8,128)(2,1)} %get-tuple-element.15) | copy-start | bytes 1572868
